TPU v7x, 32 devices: a whole 2x2x4 slice. The times are simulated.
32 devices in a mesh: parts: 2 (over x), shard: 16 (over z, y, core).
Axes of the slice: x: 2, y: 2, z: 4, core: 2. Of those that a mesh axis runs over, the one named last changes fastest.
Arguments:
- queries: bfloat16 [256, 32, 128], P(('parts', 'shard')), parts along dimension 0, may hold values from -6 to 6
- doc_tokens: bfloat16 [256, 128, 128], P(('parts', 'shard')), parts along dimension 0, may hold values from -0.5 to 0.5
- doc_lens: int32 [256], P(('parts', 'shard')), parts along dimension 0, may hold values from 1 to 128
- candidates: int32 [256, 128], P(('parts', 'shard')), parts along dimension 0, may hold values from 0 to 127
Outputs:
- scores: float32 [256, 128], P(('parts', 'shard')), parts along dimension 0
There are 2 independent parts, one for each index of `parts`. A program takes and returns all parts, laid end to end along the dimension named above; each array names one. Nothing has to cross between parts.
Inputs may be any that keep to these rules, and one draw needn't show every extreme that they name: `doc_lens`: every document has at least one live row. `candidates`: ids of documents of the same part.
All inputs are finite; a program needn't handle non-finite values.
Results may differ from a plain program's by a relative error of at most 0.0003.
Values may be sent and summed in bfloat16 or wider, within the bound.
A program may use at most 64 MiB of HBM per device.

v0:
```python
import functools

import jax
import jax.numpy as jnp
from jax import lax
from jax.experimental import pallas as pl
from jax.experimental.pallas import tpu as pltpu
from jax.sharding import PartitionSpec as P

LANES = 128
MESH = pl.DeviceIdType.MESH


def flip(index, mask):
    out = index
    bit = 1
    while bit <= mask:
        if mask & bit:
            out = out + bit - 2 * bit * ((index // bit) % 2)
        bit *= 2
    return out


def cut_points(docs):
    return [0, docs // 2, docs - docs // 4, docs]


def score_kernel(groups, tokens, lens_ref, q_hbm, d_hbm, table_ref,
                 qbuf, dbuf, best, outgoing, pieces,
                 local_sem, q_send, q_recv, p_send, p_recv, y_send, y_recv, f_send, f_recv, o_send, o_recv):
    part = lax.axis_index("parts")
    me = lax.axis_index("shard")
    k = lax.rem(me, 2)
    b = lax.rem(me // 2, 2)
    g = me // 4

    def at(g_, b_, k_):
        return (part, g_ * 4 + b_ * 2 + k_)

    docs, rows, width = d_hbm.shape
    q_rows = q_hbm.shape[0]
    count = q_rows // tokens
    edges = cut_points(docs)
    chunks = len(edges) - 1
    slots = {name: b_ * 2 + k_ for name, b_, k_ in
             (("me", b, k), ("partner", b, 1 - k), ("y", 1 - b, k), ("yp", 1 - b, 1 - k))}
    partner = at(g, b, 1 - k)
    across = at(g, 1 - b, k)
    corner = at(g, 1 - b, 1 - k)
    order = [1] + [j for j in range(groups - 1, 1, -1)]

    q_in = pltpu.make_async_copy(q_hbm, qbuf.at[g], local_sem.at[0])
    d_in = pltpu.make_async_copy(d_hbm, dbuf.at[slots["me"]], local_sem.at[1])
    d_in.start()
    q_in.start()

    barrier = pltpu.get_barrier_semaphore()
    takers = [at(flip(g, j), b, k) for j in order]
    for peer in takers + [partner, across, corner]:
        pl.semaphore_signal(barrier, inc=1, device_id=peer, device_id_type=MESH)

    d_in.wait()
    row_of = lax.broadcasted_iota(jnp.int32, (rows, width), 0)
    for j in range(docs):
        block = dbuf[slots["me"], j]
        first = jnp.broadcast_to(block[0:1, :].astype(jnp.float32), (rows, width))
        kept = jnp.where(row_of < lens_ref[j], block.astype(jnp.float32), first)
        dbuf[slots["me"], j] = kept.astype(dbuf.dtype)
    q_in.wait()
    pl.semaphore_wait(barrier, len(takers) + 3)

    def remote(src, dst, send, recv, device):
        return pltpu.make_async_remote_copy(src_ref=src, dst_ref=dst, send_sem=send, recv_sem=recv,
                                            device_id=device, device_id_type=MESH)

    def doc_chunk(name, c, send, recv, device):
        ref = dbuf.at[slots[name], pl.ds(edges[c], edges[c + 1] - edges[c])]
        return remote(ref, ref, send.at[c], recv.at[c], device)

    mine = dbuf.at[slots["me"]]
    to_partner = remote(mine, mine, p_send, p_recv, partner)
    to_across = [doc_chunk("me", c, y_send, y_recv, across) for c in range(chunks)]
    relays = [doc_chunk("y", c, f_send, f_recv, partner) for c in range(chunks - 1)]
    relays.append(doc_chunk("me", chunks - 1, f_send, f_recv, corner))
    q_out = {j: remote(qbuf.at[g], qbuf.at[g], q_send.at[j], q_recv.at[j], peer) for j, peer in zip(order, takers)}

    to_across[0].start()
    for j in order[:2]:
        q_out[j].start()
    to_partner.start()
    for j in order[2:]:
        q_out[j].start()
    for copy in to_across[1:]:
        copy.start()
    relays[-1].start()

    have = {name: 0 for name in slots}
    done = {}
    ready = []

    def dot_max(j, name, low, high):
        n = high - low
        u = flip(g, j)
        block = dbuf[slots[name], low:high].reshape(n * rows, width)
        sim = lax.dot_general(block, qbuf[u], (((1,), (1,)), ((), ())), preferred_element_type=jnp.float32)
        best[u * 4 + slots[name], low:high, :] = jnp.max(sim.reshape(n, rows, q_rows), axis=1)

    def catch_up():
        for name in slots:
            for j in ready:
                low = done.get((j, name), 0)
                if low < have[name]:
                    dot_max(j, name, low, have[name])
                    done[j, name] = have[name]

    def arrive(event):
        kind, which = event
        if kind == "q":
            q_out[which].wait_recv()
            ready.append(which)
        elif kind == "p":
            to_partner.wait_recv()
            have["partner"] = docs
        elif kind == "y":
            to_across[which].wait_recv()
            if which < chunks - 1:
                relays[which].start()
            have["y"] = edges[which + 1]
        else:
            relays[which].wait_recv()
            have["yp"] = edges[which + 1]

    ready.append(0)
    have["me"] = docs
    catch_up()
    arrive(("p", 0))
    catch_up()
    queue = [("q", j) for j in order]
    events = []
    for c in range(chunks):
        if queue:
            events.append(queue.pop(0))
        events.append(("y", c))
        if c > 0:
            events.append(("yp", c - 1))
    for event in queue:
        events.insert(len(events) - 2, event)
    events.append(("yp", chunks - 1))
    for event in events:
        arrive(event)
        catch_up()

    q_of = lax.broadcasted_iota(jnp.int32, (count, q_rows), 1) // tokens
    pick = (q_of == lax.broadcasted_iota(jnp.int32, (count, q_rows), 0)).astype(jnp.float32)
    pick = (pick * (1.0 / tokens)).astype(jnp.bfloat16)
    rest = best[...].reshape(groups * 4 * docs, q_rows)
    total = None
    for _ in range(3):
        term = rest.astype(jnp.bfloat16)
        rest = rest - term.astype(jnp.float32)
        got = lax.dot_general(pick, term, (((1,), (1,)), ((), ())), preferred_element_type=jnp.float32)
        total = got if total is None else total + got
    blocks = total.shape[1] // LANES
    for n in range(blocks):
        outgoing[n] = total[:, n * LANES:(n + 1) * LANES]

    results = [remote(outgoing, pieces.at[g], o_send.at[i], o_recv.at[i], peer) for i, peer in enumerate(takers)]
    for copy in results[::-1]:
        copy.start()
    pieces[g] = outgoing[...]
    for copy in to_across + relays + [to_partner] + list(q_out.values()):
        copy.wait_send()

    per_unit = 4 * docs
    inside = LANES // per_unit
    lane = lax.broadcasted_iota(jnp.int32, (count, LANES), 1) // per_unit
    for copy in results:
        copy.wait_recv()
    for n in range(table_ref.shape[1] // LANES):
        total = None
        for i in range(inside):
            shift = lax.rem(i - lax.rem(g, inside) + inside, inside) * per_unit
            got = pltpu.roll(pieces[n * inside + i, g // inside], shift, 1)
            total = got if total is None else jnp.where(lane == i, got, total)
        table_ref[:, n * LANES:(n + 1) * LANES] = total
    for copy in results:
        copy.wait_send()


def gather_kernel(table_ref, cand_ref, out_ref):
    cand = cand_ref[...]
    inside = lax.rem(cand, LANES)
    which = cand // LANES
    out = None
    for n in range(table_ref.shape[1] // LANES):
        got = jnp.take_along_axis(table_ref[:, n * LANES:(n + 1) * LANES], inside, axis=1,
                                  mode="promise_in_bounds")
        out = got if out is None else jnp.where(which == n, got, out)
    out_ref[...] = out


def body(shards, queries, doc_tokens, doc_lens, candidates):
    count, tokens, width = queries.shape
    docs, rows, _ = doc_tokens.shape
    groups = shards // 4
    chunks = len(cut_points(docs)) - 1
    q_rows = count * tokens
    blocks = groups * 4 * docs // LANES
    dma = pltpu.SemaphoreType.DMA
    table = pl.pallas_call(
        functools.partial(score_kernel, groups, tokens),
        out_shape=jax.ShapeDtypeStruct((count, shards * docs), jnp.float32),
        in_specs=[
            pl.BlockSpec(memory_space=pltpu.SMEM),
            pl.BlockSpec(memory_space=pl.ANY),
            pl.BlockSpec(memory_space=pl.ANY),
        ],
        out_specs=pl.BlockSpec(memory_space=pltpu.VMEM),
        scratch_shapes=[
            pltpu.VMEM((groups, q_rows, width), queries.dtype),
            pltpu.VMEM((4, docs, rows, width), doc_tokens.dtype),
            pltpu.VMEM((groups * 4, docs, q_rows), jnp.float32),
            pltpu.VMEM((blocks, count, LANES), jnp.float32),
            pltpu.VMEM((groups, blocks, count, LANES), jnp.float32),
            dma((2,)),
            dma((groups,)), dma((groups,)),
            dma, dma,
            dma((chunks,)), dma((chunks,)),
            dma((chunks,)), dma((chunks,)),
            dma((groups,)), dma((groups,)),
        ],
        compiler_params=pltpu.CompilerParams(collective_id=0, has_side_effects=True),
    )(doc_lens, queries.reshape(q_rows, width), doc_tokens)
    return pl.pallas_call(
        gather_kernel,
        out_shape=jax.ShapeDtypeStruct(candidates.shape, jnp.float32),
    )(table, candidates)


def solution(mesh):
    in_specs = (
        P(("parts", "shard"), None, None),
        P(("parts", "shard"), None, None),
        P(("parts", "shard")),
        P(("parts", "shard"), None),
    )
    out_specs = P(("parts", "shard"), None)
    step = functools.partial(body, mesh.shape["shard"])
    return jax.shard_map(step, mesh=mesh, in_specs=in_specs, out_specs=out_specs, check_vma=False)
```

profile of v0, /device:TPU:0, one launch (start us, length us, event | category | flops | bytes accessed | tf_op | source)
XLA Modules:
  0.0 20.6 jit_solution(12994275288792187934)
XLA Ops:
  0.0 19.3 %shard_map.46.table_ref = f32[8,128]{1,0:T(8,128)} custom-call(s32[8]{0:T(128)} %lens_ref.1, bf16[256,128]{1,0:T(8,128)(2,1)} %bitcast.1, bf16[8,128,128]{2,1,0:T(8,128)(2,1)} %d_hbm.1), custom_call_target="tpu_custom_call" | custom-call | tf_op jit(solution)/shard_map/pallas_call | solution.py:210
  19.3 1.4 %shard_map.47 = f32[8,128]{1,0:T(8,128)} custom-call(f32[8,128]{1,0:T(8,128)} %shard_map.46.table_ref, s32[8,128]{1,0:T(8,128)} %cand_ref.1), custom_call_target="tpu_custom_call" | custom-call | tf_op jit(solution)/shard_map/pallas_call | solution.py:234
where the time goes:
time: 20.8 us; the launch traced here: 20.6 us
  Pallas kernels  20.6 us (99%)
    pallas_call x1, Pallas kernels, body(): pl.pallas_call(functools.partial(score_kernel, groups, tokens), out_shape...  19.3 us
    pallas_call x1, Pallas kernels, body(): pl.pallas_call(gather_kernel, out_shape=jax.ShapeDtypeStruct(candidates.s...  1.36 us

commit v1 on v0

--- a/solution.py
+++ b/solution.py
@@ -25,8 +25,8 @@
     return [0, docs // 2, docs - docs // 4, docs]
 
 
-def score_kernel(groups, tokens, lens_ref, q_hbm, d_hbm, table_ref,
-                 qbuf, dbuf, best, outgoing, pieces,
+def score_kernel(groups, tokens, lens_hbm, q_hbm, d_hbm, cand_hbm, out_ref,
+                 lens_ref, cand_ref, qbuf, dbuf, best, outgoing, pieces,
                  local_sem, q_send, q_recv, p_send, p_recv, y_send, y_recv, f_send, f_recv, o_send, o_recv):
     part = lax.axis_index("parts")
     me = lax.axis_index("shard")
@@ -51,14 +51,19 @@
 
     q_in = pltpu.make_async_copy(q_hbm, qbuf.at[g], local_sem.at[0])
     d_in = pltpu.make_async_copy(d_hbm, dbuf.at[slots["me"]], local_sem.at[1])
+    lens_in = pltpu.make_async_copy(lens_hbm, lens_ref, local_sem.at[2])
+    cand_in = pltpu.make_async_copy(cand_hbm, cand_ref, local_sem.at[3])
+    lens_in.start()
     d_in.start()
     q_in.start()
+    cand_in.start()
 
     barrier = pltpu.get_barrier_semaphore()
     takers = [at(flip(g, j), b, k) for j in order]
     for peer in takers + [partner, across, corner]:
         pl.semaphore_signal(barrier, inc=1, device_id=peer, device_id_type=MESH)
 
+    lens_in.wait()
     d_in.wait()
     row_of = lax.broadcasted_iota(jnp.int32, (rows, width), 0)
     for j in range(docs):
@@ -174,29 +179,24 @@
     per_unit = 4 * docs
     inside = LANES // per_unit
     lane = lax.broadcasted_iota(jnp.int32, (count, LANES), 1) // per_unit
+    cand_in.wait()
+    cand = cand_ref[...]
+    inside_of = lax.rem(cand, LANES)
+    tile_of = cand // LANES
+    out = None
     for copy in results:
         copy.wait_recv()
-    for n in range(table_ref.shape[1] // LANES):
+    for n in range(groups * 4 * docs // LANES):
         total = None
         for i in range(inside):
             shift = lax.rem(i - lax.rem(g, inside) + inside, inside) * per_unit
             got = pltpu.roll(pieces[n * inside + i, g // inside], shift, 1)
             total = got if total is None else jnp.where(lane == i, got, total)
-        table_ref[:, n * LANES:(n + 1) * LANES] = total
+        got = jnp.take_along_axis(total, inside_of, axis=1, mode="promise_in_bounds")
+        out = got if out is None else jnp.where(tile_of == n, got, out)
+    out_ref[...] = out
     for copy in results:
         copy.wait_send()
-
-
-def gather_kernel(table_ref, cand_ref, out_ref):
-    cand = cand_ref[...]
-    inside = lax.rem(cand, LANES)
-    which = cand // LANES
-    out = None
-    for n in range(table_ref.shape[1] // LANES):
-        got = jnp.take_along_axis(table_ref[:, n * LANES:(n + 1) * LANES], inside, axis=1,
-                                  mode="promise_in_bounds")
-        out = got if out is None else jnp.where(which == n, got, out)
-    out_ref[...] = out
 
 
 def body(shards, queries, doc_tokens, doc_lens, candidates):
@@ -207,22 +207,20 @@
     q_rows = count * tokens
     blocks = groups * 4 * docs // LANES
     dma = pltpu.SemaphoreType.DMA
-    table = pl.pallas_call(
+    return pl.pallas_call(
         functools.partial(score_kernel, groups, tokens),
-        out_shape=jax.ShapeDtypeStruct((count, shards * docs), jnp.float32),
-        in_specs=[
-            pl.BlockSpec(memory_space=pltpu.SMEM),
-            pl.BlockSpec(memory_space=pl.ANY),
-            pl.BlockSpec(memory_space=pl.ANY),
-        ],
+        out_shape=pltpu.VMEM(candidates.shape, jnp.float32),
+        in_specs=[pl.BlockSpec(memory_space=pl.ANY)] * 4,
         out_specs=pl.BlockSpec(memory_space=pltpu.VMEM),
         scratch_shapes=[
+            pltpu.SMEM(doc_lens.shape, jnp.int32),
+            pltpu.VMEM(candidates.shape, jnp.int32),
             pltpu.VMEM((groups, q_rows, width), queries.dtype),
             pltpu.VMEM((4, docs, rows, width), doc_tokens.dtype),
             pltpu.VMEM((groups * 4, docs, q_rows), jnp.float32),
             pltpu.VMEM((blocks, count, LANES), jnp.float32),
             pltpu.VMEM((groups, blocks, count, LANES), jnp.float32),
-            dma((2,)),
+            dma((4,)),
             dma((groups,)), dma((groups,)),
             dma, dma,
             dma((chunks,)), dma((chunks,)),
@@ -230,11 +228,7 @@
             dma((groups,)), dma((groups,)),
         ],
         compiler_params=pltpu.CompilerParams(collective_id=0, has_side_effects=True),
-    )(doc_lens, queries.reshape(q_rows, width), doc_tokens)
-    return pl.pallas_call(
-        gather_kernel,
-        out_shape=jax.ShapeDtypeStruct(candidates.shape, jnp.float32),
-    )(table, candidates)
+    )(doc_lens, queries.reshape(q_rows, width), doc_tokens, candidates)
 
 
 def solution(mesh):

time: 20.8 us -> 18.8 us (0.904)
  Pallas kernels: 20.6 us -> 18 us
  local copies, waits for them, and re-layouts: 0 us -> 0.6 us
    pallas_call x1 -> x0, Pallas kernels: 1.36 us -> none  [body(): pl.pallas_call(gather_kernel, out_shape=jax.ShapeDtypeStruct(candidates.s...]
    pallas_call x1, Pallas kernels: 19.3 us -> 18 us  [body(): pl.pallas_call(functools.partial(score_kernel, groups, tokens), out_shape...]
    unnamed x0 -> x1, local copies, waits for them, and re-layouts: none -> 0.6 us
where the time goes in v1:
time: 18.8 us; the launch traced here: 18.6 us
  Pallas kernels  18 us (96%)
  local copies, waits for them, and re-layouts  0.6 us (3%)
    pallas_call x1, Pallas kernels, body(): pl.pallas_call(functools.partial(score_kernel, groups, tokens), out_shape...  18 us
    unnamed x1, local copies, waits for them, and re-layouts  0.6 us

profile of v1, /device:TPU:0, one launch (start us, length us, event | category | flops | bytes accessed | tf_op | source)
XLA Modules:
  0.0 18.6 jit_solution(1443047274138286262)
XLA Ops:
  0.0 18.0 %shard_map.46 = f32[8,128]{1,0:T(8,128)S(1)} custom-call(s32[8]{0:T(128)} %lens_hbm.1, bf16[256,128]{1,0:T(8,128)(2,1)} %bitcast.1, bf16[8,128,128]{2,1,0:T(8,128)(2,1)} %d_hbm.1, s32[8,128]{1,0:T(8,128)} %cand_hbm.1), custom_call_target="tpu_custom_call" | custom-call | tf_op jit(solution)/shard_map/pallas_call | solution.py:210
  18.0 0.6 %copy.6 = f32[8,128]{1,0:T(8,128)} copy(f32[8,128]{1,0:T(8,128)S(1)} %shard_map.46) | data formatting | bytes 8192

commit v2 on v1

v2 whole, which is shorter than its diff:
```python
import functools

import jax
import jax.numpy as jnp
from jax import lax
from jax.experimental import pallas as pl
from jax.experimental.pallas import tpu as pltpu
from jax.sharding import PartitionSpec as P

LANES = 128
MESH = pl.DeviceIdType.MESH


def flip(index, mask):
    out = index
    bit = 1
    while bit <= mask:
        if mask & bit:
            out = out + bit - 2 * bit * ((index // bit) % 2)
        bit *= 2
    return out


def cut_points(docs):
    return [0, docs // 2, docs - docs // 4, docs]


def score_kernel(groups, tokens, lens_hbm, q_hbm, d_hbm, cand_hbm, out_ref,
                 lens_ref, cand_ref, qbuf, dbuf, best, outgoing, pieces,
                 local_sem, here, q_send, q_recv, p_send, p_recv, y_send, y_recv, f_send, f_recv, o_send, o_recv):
    part = lax.axis_index("parts")
    me = lax.axis_index("shard")
    k = lax.rem(me, 2)
    b = lax.rem(me // 2, 2)
    g = me // 4

    def at(g_, b_, k_):
        return (part, g_ * 4 + b_ * 2 + k_)

    docs, rows, width = d_hbm.shape
    q_rows = q_hbm.shape[0]
    count = q_rows // tokens
    per_unit = 4 * docs
    edges = cut_points(docs)
    chunks = len(edges) - 1
    order = list(range(1, groups))
    end = lax.rem(g + 1, 4) < 2
    mask = {j: jnp.where(end, j, j ^ 1) if j % 4 > 1 else j for j in order}
    other = {j: jnp.where(end, flip(g, j), flip(g, j ^ 1)) if j % 4 > 1 else flip(g, j) for j in order}
    other[0] = g
    partner = at(g, b, 1 - k)
    across = at(g, 1 - b, 1 - k)
    level = {j: at(other[j], b, 1 - k) for j in order}

    def remote(src, dst, send, recv, device):
        return pltpu.make_async_remote_copy(src_ref=src, dst_ref=dst, send_sem=send, recv_sem=recv,
                                            device_id=device, device_id_type=MESH)

    lens_in = pltpu.make_async_copy(lens_hbm, lens_ref, local_sem.at[0])
    q_in = pltpu.make_async_copy(q_hbm, qbuf.at[g], local_sem.at[1])
    cand_in = pltpu.make_async_copy(cand_hbm, cand_ref, local_sem.at[2])
    d_in = pltpu.make_async_copy(d_hbm, dbuf.at[0], local_sem.at[3])
    lens_in.start()
    d_in.start()
    q_in.start()
    cand_in.start()

    pairs = [(0, partner, k == 1), (1, across, b == 0)] + [(1 + mask[j], level[j], g < other[j]) for j in order]
    barrier = pltpu.get_barrier_semaphore()
    greeted = 0
    for _, peer, first in pairs:
        greeted = greeted + jnp.where(first, 0, 1)

        @pl.when(first)
        def _():
            pl.semaphore_signal(barrier, inc=1, device_id=peer, device_id_type=MESH)

    @pl.when(greeted > 0)
    def _():
        pl.semaphore_wait(barrier, greeted)

    for slot, peer, first in pairs:
        @pl.when(jnp.logical_not(first))
        def _():
            pl.semaphore_signal(here.at[slot], inc=1, device_id=peer, device_id_type=MESH)

    def meet(which):
        slot, _, first = pairs[which]

        @pl.when(first)
        def _():
            pl.semaphore_wait(here.at[slot], 1)

    mine = qbuf.at[g]
    q_out = {j: remote(mine, mine, q_send.at[mask[j]], q_recv.at[mask[j]], level[j]) for j in order}
    to_partner = remote(dbuf.at[0], dbuf.at[1], p_send, p_recv, partner)
    to_across, relays = [], []
    for c in range(chunks):
        span = pl.ds(edges[c], edges[c + 1] - edges[c])
        to_across.append(remote(dbuf.at[0, span], dbuf.at[2, span], y_send.at[c], y_recv.at[c], across))
        relays.append(remote(dbuf.at[2, span], dbuf.at[3, span], f_send.at[c], f_recv.at[c], partner))

    lens_in.wait()
    d_in.wait()
    row_of = lax.broadcasted_iota(jnp.int32, (rows, width), 0)
    for c in range(chunks):
        for j in range(edges[c], edges[c + 1]):
            block = dbuf[0, j]
            first_row = jnp.broadcast_to(block[0:1, :].astype(jnp.float32), (rows, width))
            kept = jnp.where(row_of < lens_ref[j], block.astype(jnp.float32), first_row)
            dbuf[0, j] = kept.astype(dbuf.dtype)
        if c == 0:
            meet(1)
        to_across[c].start()
    meet(0)
    to_partner.start()
    q_in.wait()

    have = [docs, 0, 0, 0]
    done = {}
    ready = []

    def dot_max(unit, which, low, high):
        block = qbuf[other[unit]]
        for j in range(low, high):
            sim = lax.dot_general(dbuf[which, j], block, (((1,), (1,)), ((), ())), preferred_element_type=jnp.float32)
            best[other[unit], which * docs + j:which * docs + j + 1, :] = jnp.max(sim, axis=0, keepdims=True)

    def catch_up():
        for which in range(4):
            for unit in ready:
                low = done.get((unit, which), 0)
                if low < have[which]:
                    dot_max(unit, which, low, have[which])
                    done[unit, which] = have[which]

    if order:
        meet(2)
        q_out[order[0]].start()
    ready.append(0)
    catch_up()
    for i, j in enumerate(order[1:]):
        meet(3 + i)
        q_out[j].start()

    cand_in.wait()
    cand = cand_ref[...]
    device = cand // docs
    same = lax.rem(device // 2, 2) == b
    source = device // 4
    holder = jnp.where(source == g, k, 1 - k)
    near = lax.rem(device, 2) == holder
    local = jnp.where(same, jnp.where(near, 0, docs), jnp.where(near, 3 * docs, 2 * docs))
    lane = lax.rem(g * per_unit, LANES) + lax.rem(cand, docs) + local

    def arrive(event):
        kind, which = event
        if kind == "p":
            to_partner.wait_recv()
            have[1] = docs
        elif kind == "q":
            q_out[which].wait_recv()
            ready.append(which)
        elif kind == "y":
            to_across[which].wait_recv()
            relays[which].start()
            have[2] = edges[which + 1]
        else:
            relays[which].wait_recv()
            have[3] = edges[which + 1]

    events = [(("p", 0), True)]
    for i in range(max(len(order), chunks)):
        if i < chunks and i:
            events += [(("r", i - 1), i == 1), (("y", i), i == 1)]
        if i < len(order):
            events.append((("q", order[i]), True))
        if i < chunks and not i:
            events.append((("y", i), True))
    events.append((("r", chunks - 1), True))
    for event, now in events:
        arrive(event)
        if now:
            catch_up()

    q_of = lax.broadcasted_iota(jnp.int32, (count, q_rows), 1) // tokens
    pick = (q_of == lax.broadcasted_iota(jnp.int32, (count, q_rows), 0)).astype(jnp.float32)
    pick = (pick * (1.0 / tokens)).astype(jnp.bfloat16)
    rest = best[...].reshape(groups * per_unit, q_rows)
    total = None
    for _ in range(2):
        term = rest.astype(jnp.bfloat16)
        rest = rest - term.astype(jnp.float32)
        got = lax.dot_general(pick, term, (((1,), (1,)), ((), ())), preferred_element_type=jnp.float32)
        total = got if total is None else total + got
    for n in range(total.shape[1] // LANES):
        outgoing[n] = total[:, n * LANES:(n + 1) * LANES]

    results = {}
    for j in order:
        results[j] = remote(outgoing.at[other[j] * per_unit // LANES], pieces.at[g], o_send.at[mask[j]],
                            o_recv.at[mask[j]], level[j])
    for copy in list(results.values())[::-1]:
        copy.start()

    def picked(piece):
        return jnp.take_along_axis(piece, lane, axis=1, mode="promise_in_bounds")

    out = picked(outgoing[g * per_unit // LANES])
    for copy in to_across + relays + [to_partner] + list(q_out.values()):
        copy.wait_send()
    for j, copy in results.items():
        copy.wait_recv()
        out = jnp.where(source == other[j], picked(pieces[other[j]]), out)
    out_ref[...] = out
    for copy in results.values():
        copy.wait_send()


def body(shards, queries, doc_tokens, doc_lens, candidates):
    count, tokens, width = queries.shape
    docs, rows, _ = doc_tokens.shape
    groups = shards // 4
    chunks = len(cut_points(docs)) - 1
    q_rows = count * tokens
    blocks = groups * 4 * docs // LANES
    dma = pltpu.SemaphoreType.DMA
    return pl.pallas_call(
        functools.partial(score_kernel, groups, tokens),
        out_shape=pltpu.VMEM(candidates.shape, jnp.float32),
        in_specs=[pl.BlockSpec(memory_space=pl.ANY)] * 4,
        out_specs=pl.BlockSpec(memory_space=pltpu.VMEM),
        scratch_shapes=[
            pltpu.SMEM(doc_lens.shape, jnp.int32),
            pltpu.VMEM(candidates.shape, jnp.int32),
            pltpu.VMEM((groups, q_rows, width), queries.dtype),
            pltpu.VMEM((4, docs, rows, width), doc_tokens.dtype),
            pltpu.VMEM((groups, 4 * docs, q_rows), jnp.float32),
            pltpu.VMEM((blocks, count, LANES), jnp.float32),
            pltpu.VMEM((groups, count, LANES), jnp.float32),
            dma((4,)),
            pltpu.SemaphoreType.REGULAR((groups + 1,)),
            dma((groups,)), dma((groups,)),
            dma, dma,
            dma((chunks,)), dma((chunks,)),
            dma((chunks,)), dma((chunks,)),
            dma((groups,)), dma((groups,)),
        ],
        compiler_params=pltpu.CompilerParams(collective_id=0, has_side_effects=True),
    )(doc_lens, queries.reshape(q_rows, width), doc_tokens, candidates)


def solution(mesh):
    in_specs = (
        P(("parts", "shard"), None, None),
        P(("parts", "shard"), None, None),
        P(("parts", "shard")),
        P(("parts", "shard"), None),
    )
    out_specs = P(("parts", "shard"), None)
    step = functools.partial(body, mesh.shape["shard"])
    return jax.shard_map(step, mesh=mesh, in_specs=in_specs, out_specs=out_specs, check_vma=False)
```

time: 18.8 us -> 17.9 us (0.952)
  Pallas kernels: 18 us -> 17.1 us
    pallas_call x1, Pallas kernels: 18 us -> 17.1 us  [body(): pl.pallas_call(functools.partial(score_kernel, groups, tokens), out_shape...]
where the time goes in v2:
time: 17.9 us; the launch traced here: 17.7 us
  Pallas kernels  17.1 us (96%)
  local copies, waits for them, and re-layouts  0.6 us (3%)
    pallas_call x1, Pallas kernels, body(): pl.pallas_call(functools.partial(score_kernel, groups, tokens), out_shape...  17.1 us
    unnamed x1, local copies, waits for them, and re-layouts  0.6 us

profile of v2, /device:TPU:0, one launch (start us, length us, event | category | flops | bytes accessed | tf_op | source)
XLA Modules:
  0.0 17.7 jit_solution(11283161298672811065)
XLA Ops:
  0.0 17.1 %shard_map.46 = f32[8,128]{1,0:T(8,128)S(1)} custom-call(s32[8]{0:T(128)} %lens_hbm.1, bf16[256,128]{1,0:T(8,128)(2,1)} %bitcast.1, bf16[8,128,128]{2,1,0:T(8,128)(2,1)} %d_hbm.1, s32[8,128]{1,0:T(8,128)} %cand_hbm.1), custom_call_target="tpu_custom_call" | custom-call | tf_op jit(solution)/shard_map/pallas_call | solution.py:228
  17.2 0.6 %copy.6 = f32[8,128]{1,0:T(8,128)} copy(f32[8,128]{1,0:T(8,128)S(1)} %shard_map.46) | data formatting | bytes 8192

commit v3 on v2

v3 whole, which is shorter than its diff:
```python
import functools

import jax
import jax.numpy as jnp
from jax import lax
from jax.experimental import pallas as pl
from jax.experimental.pallas import tpu as pltpu
from jax.sharding import PartitionSpec as P

LANES = 128
MESH = pl.DeviceIdType.MESH


def flip(index, mask):
    out = index
    bit = 1
    while bit <= mask:
        if mask & bit:
            out = out + bit - 2 * bit * ((index // bit) % 2)
        bit *= 2
    return out


def cut_points(docs):
    return [0, docs // 2, docs - docs // 4, docs]


def score_kernel(groups, tokens, lens_hbm, q_hbm, d_hbm, cand_hbm, out_ref,
                 lens_ref, cand_ref, qbuf, dbuf, hbuf, best, rest_best, outgoing, pieces, extra,
                 local_sem, here, q_send, q_recv, d_send, p_recv, y_recv, f_recv, o_send, o_recv, h_send, h_recv):
    part = lax.axis_index("parts")
    me = lax.axis_index("shard")
    k = lax.rem(me, 2)
    b = lax.rem(me // 2, 2)
    g = me // 4

    def at(g_, b_, k_):
        return (part, g_ * 4 + b_ * 2 + k_)

    docs, rows, width = d_hbm.shape
    q_rows = q_hbm.shape[0]
    count = q_rows // tokens
    per_unit = 4 * docs
    edges = cut_points(docs)
    chunks = len(edges) - 1
    order = list(range(1, groups))
    end = lax.rem(g, 4) == 0
    mask = {j: jnp.where(end, j, j ^ 1) if j % 4 > 1 else j for j in order}
    other = {j: jnp.where(end, flip(g, j), flip(g, j ^ 1)) if j % 4 > 1 else flip(g, j) for j in order}
    other[0] = g
    partner = at(g, b, 1 - k)
    across = at(g, 1 - b, 1 - k)
    level = {j: at(other[j], b, 1 - k) for j in order}

    short = groups % 4 == 0
    late = edges[-2]
    tail = docs - late
    home = jnp.logical_and(lax.rem(g, 4) == 0, b == 0)
    sooner = jnp.logical_and(lax.rem(g, 4) == 3, b == 0)
    giver = jnp.logical_and(lax.rem(g, 4) == 3, b == 1)
    top = flip(g, 3)

    def remote(src, dst, send, recv, device):
        return pltpu.make_async_remote_copy(src_ref=src, dst_ref=dst, send_sem=send, recv_sem=recv,
                                            device_id=device, device_id_type=MESH)

    lens_in = pltpu.make_async_copy(lens_hbm, lens_ref, local_sem.at[0])
    q_in = pltpu.make_async_copy(q_hbm, qbuf.at[g], local_sem.at[1])
    cand_in = pltpu.make_async_copy(cand_hbm, cand_ref, local_sem.at[2])
    d_in = pltpu.make_async_copy(d_hbm, dbuf.at[0], local_sem.at[3])
    lens_in.start()
    d_in.start()
    q_in.start()
    cand_in.start()

    pairs = [(0, partner, k == 1), (1, across, b == 0)] + [(1 + mask[j], level[j], g < other[j]) for j in order]
    barrier = pltpu.get_barrier_semaphore()
    greeted = 0
    for _, peer, first in pairs:
        greeted = greeted + jnp.where(first, 0, 1)

        @pl.when(first)
        def _():
            pl.semaphore_signal(barrier, inc=1, device_id=peer, device_id_type=MESH)

    if short:
        greeted = greeted + jnp.where(giver, 1, 0)

        @pl.when(home)
        def _():
            pl.semaphore_signal(barrier, inc=1, device_id=at(top, 1, 1 - k), device_id_type=MESH)

    @pl.when(greeted > 0)
    def _():
        pl.semaphore_wait(barrier, greeted)

    for slot, peer, first in pairs:
        @pl.when(jnp.logical_not(first))
        def _():
            pl.semaphore_signal(here.at[slot], inc=1, device_id=peer, device_id_type=MESH)

    def meet(which):
        slot, _, first = pairs[which]

        @pl.when(first)
        def _():
            pl.semaphore_wait(here.at[slot], 1)

    mine = qbuf.at[g]
    q_out = {j: remote(mine, mine, q_send, q_recv.at[mask[j] - 1], level[j]) for j in order}
    to_partner = remote(dbuf.at[0], dbuf.at[1], d_send, p_recv, partner)
    to_across, relays = [], []
    for c in range(chunks):
        span = pl.ds(edges[c], edges[c + 1] - edges[c])
        to_across.append(remote(dbuf.at[0, span], dbuf.at[2, span], d_send, y_recv.at[c], across))
        relays.append(remote(dbuf.at[2, span], dbuf.at[3, span], d_send, f_recv.at[c], partner))

    lens_in.wait()
    d_in.wait()
    row_of = lax.broadcasted_iota(jnp.int32, (rows, width), 0)
    for c in range(chunks):
        for j in range(edges[c], edges[c + 1]):
            block = dbuf[0, j]
            first_row = jnp.broadcast_to(block[0:1, :].astype(jnp.float32), (rows, width))
            kept = jnp.where(row_of < lens_ref[j], block.astype(jnp.float32), first_row)
            dbuf[0, j] = kept.astype(dbuf.dtype)
        if c == 0:
            meet(1)
        to_across[c].start()
    meet(0)
    to_partner.start()
    q_in.wait()

    def dot_max(unit, which, low, high):
        block = qbuf[other[unit]]
        for j in range(low, high):
            sim = lax.dot_general(dbuf[which, j], block, (((1,), (1,)), ((), ())), preferred_element_type=jnp.float32)
            best[other[unit], which * docs + j:which * docs + j + 1, :] = jnp.max(sim, axis=0, keepdims=True)

    def catch_up(have, ready, done):
        for which in range(4):
            for unit in ready:
                low = done.get((unit, which), 0)
                if low < have[which]:
                    dot_max(unit, which, low, have[which])
                    done[unit, which] = have[which]

    if order:
        meet(2)
        q_out[order[0]].start()
    dot_max(0, 0, 0, docs)
    for i, j in enumerate(order[1:]):
        meet(3 + i)
        q_out[j].start()

    give = remote(dbuf.at[0, pl.ds(late, tail)], hbuf.at[0], h_send, h_recv.at[0], at(top, 0, 1 - k))
    share = remote(hbuf.at[0], hbuf.at[1], h_send, h_recv.at[1], partner)
    cand_in.wait()
    cand = cand_ref[...]
    device = cand // docs
    same = lax.rem(device // 2, 2) == b
    source = device // 4
    holder = jnp.where(source == g, k, 1 - k)
    near = lax.rem(device, 2) == holder
    local = jnp.where(same, jnp.where(near, 0, docs), jnp.where(near, 3 * docs, 2 * docs))
    lane = lax.rem(cand, docs) + local

    q_of = lax.broadcasted_iota(jnp.int32, (count, q_rows), 1) // tokens
    pick = (q_of == lax.broadcasted_iota(jnp.int32, (count, q_rows), 0)).astype(jnp.float32)
    pick = (pick * (1.0 / tokens)).astype(jnp.bfloat16)

    def means(rest):
        total = None
        for _ in range(2):
            term = rest.astype(jnp.bfloat16)
            rest = rest - term.astype(jnp.float32)
            got = lax.dot_general(pick, term, (((1,), (1,)), ((), ())), preferred_element_type=jnp.float32)
            total = got if total is None else total + got
        return total

    def widened(few):
        return jnp.concatenate([few, jnp.zeros((count, LANES - few.shape[1]), jnp.float32)], axis=1)

    results = {j: remote(outgoing.at[j], pieces.at[g], o_send, o_recv, level[j]) for j in order}

    def run(plan):
        have, ready, done = [docs, 0, 0, 0], [0], {(0, 0): docs}
        for kind, which, now in plan:
            if kind == "p":
                to_partner.wait_recv()
                have[1] = docs
            elif kind == "q":
                q_out[which].wait_recv()
                ready.append(which)
            elif kind == "y":
                to_across[which].wait_recv()
                relays[which].start()
                have[2] = edges[which + 1]
            elif kind == "r":
                relays[which].wait_recv()
                have[3] = edges[which + 1]
            elif kind == "give":
                @pl.when(giver)
                def _():
                    give.start()
            else:
                def answer():
                    outgoing[which] = widened(means(best[other[which]]))
                    if which:
                        results[which].start()

                if kind == "soon":
                    pl.when(sooner)(answer)
                elif short and which == 2 and now:
                    pl.when(jnp.logical_not(sooner))(answer)
                else:
                    answer()
                continue
            if now:
                catch_up(have, ready, done)

    docs_first = [("p", 0, True)] + [("q", j, True) for j in order[:1]]
    for c in range(chunks):
        docs_first += [("y", c, True)] + [("r", c - 1, True)] * (c > 0)
    docs_first.append(("r", chunks - 1, True))
    docs_first += [("s", j, False) for j in order[:1]]
    for j in order[1:]:
        docs_first += [("q", j, True), ("s", j, False)]
    docs_first.append(("s", 0, False))
    docs_last = [("p", 0, True)]
    for i in range(max(len(order), chunks)):
        if i < chunks and i:
            docs_last += [("r", i - 1, True)]
            if short and i == chunks - 1:
                docs_last += [("soon", 2, True)]
            docs_last += [("y", i, i == 1)]
        if i < len(order):
            docs_last.append(("q", order[i], True))
        if i < chunks and not i:
            docs_last += [("y", i, True)] + [("give", 0, False)] * short
    docs_last.append(("r", chunks - 1, True))
    docs_last += [("s", j, True) for j in order[::-1] + [0]]
    low = lax.rem(g, 4) < 2

    @pl.when(low)
    def _():
        run(docs_first)

    @pl.when(jnp.logical_not(low))
    def _():
        run(docs_last)

    if short:
        @pl.when(home)
        def _():
            give.wait_recv()
            share.start()
            for n in range(2):
                if n:
                    share.wait_recv()
                for j in range(tail):
                    sim = lax.dot_general(hbuf[n, j], qbuf[g], (((1,), (1,)), ((), ())), preferred_element_type=jnp.float32)
                    rest_best[n * tail + j:n * tail + j + 1, :] = jnp.max(sim, axis=0, keepdims=True)
            extra[...] = widened(means(rest_best[...]))

        @pl.when(jnp.logical_or(home, giver))
        def _():
            give.wait_send()

    def picked(piece, lanes):
        return jnp.take_along_axis(piece, lanes, axis=1, mode="promise_in_bounds")

    sent = [remote(dbuf.at[pl.ds(0, 3)], dbuf.at[pl.ds(0, 3)], d_send, p_recv, partner)]
    if order:
        sent.append(remote(qbuf.at[pl.ds(0, groups - 1)], qbuf.at[pl.ds(0, groups - 1)], q_send, p_recv, partner))
    out = picked(outgoing[0], lane)
    for copy in sent:
        copy.wait_send()
    if order:
        back = remote(pieces.at[pl.ds(0, groups - 1)], pieces.at[pl.ds(0, groups - 1)], o_send, o_recv, partner)
        back.wait_recv()
        for j in order:
            out = jnp.where(source == other[j], picked(pieces[other[j]], lane), out)
        back.wait_send()
    if short:
        row = lax.rem(cand, docs) - late
        whole = (source == top) & jnp.logical_not(same) & (row >= 0) & home
        out = jnp.where(whole, picked(extra[...], jnp.where(whole, row + jnp.where(near, 0, tail), 0)), out)
    out_ref[...] = out


def body(shards, queries, doc_tokens, doc_lens, candidates):
    count, tokens, width = queries.shape
    docs, rows, _ = doc_tokens.shape
    groups = shards // 4
    chunks = len(cut_points(docs)) - 1
    tail = docs - cut_points(docs)[-2]
    q_rows = count * tokens
    dma = pltpu.SemaphoreType.DMA
    return pl.pallas_call(
        functools.partial(score_kernel, groups, tokens),
        out_shape=pltpu.VMEM(candidates.shape, jnp.float32),
        in_specs=[pl.BlockSpec(memory_space=pl.ANY)] * 4,
        out_specs=pl.BlockSpec(memory_space=pltpu.VMEM),
        scratch_shapes=[
            pltpu.SMEM(doc_lens.shape, jnp.int32),
            pltpu.VMEM(candidates.shape, jnp.int32),
            pltpu.VMEM((groups, q_rows, width), queries.dtype),
            pltpu.VMEM((4, docs, rows, width), doc_tokens.dtype),
            pltpu.VMEM((2, tail, rows, width), doc_tokens.dtype),
            pltpu.VMEM((groups, 4 * docs, q_rows), jnp.float32),
            pltpu.VMEM((2 * tail, q_rows), jnp.float32),
            pltpu.VMEM((groups, count, LANES), jnp.float32),
            pltpu.VMEM((groups, count, LANES), jnp.float32),
            pltpu.VMEM((count, LANES), jnp.float32),
            dma((4,)),
            pltpu.SemaphoreType.REGULAR((groups + 1,)),
            dma, dma((groups - 1,)),
            dma, dma, dma((chunks,)), dma((chunks,)),
            dma, dma,
            dma, dma((2,)),
        ],
        compiler_params=pltpu.CompilerParams(collective_id=0, has_side_effects=True),
    )(doc_lens, queries.reshape(q_rows, width), doc_tokens, candidates)


def solution(mesh):
    in_specs = (
        P(("parts", "shard"), None, None),
        P(("parts", "shard"), None, None),
        P(("parts", "shard")),
        P(("parts", "shard"), None),
    )
    out_specs = P(("parts", "shard"), None)
    step = functools.partial(body, mesh.shape["shard"])
    return jax.shard_map(step, mesh=mesh, in_specs=in_specs, out_specs=out_specs, check_vma=False)
```

time: 17.9 us -> 17.1 us (0.955)
  Pallas kernels: 17.1 us -> 16.3 us
    pallas_call x1, Pallas kernels: 17.1 us -> 16.3 us  [body(): pl.pallas_call(functools.partial(score_kernel, groups, tokens), out_shape...]
where the time goes in v3:
time: 17.1 us; the launch traced here: 16.9 us
  Pallas kernels  16.3 us (95%)
  local copies, waits for them, and re-layouts  0.6 us (4%)
    pallas_call x1, Pallas kernels, body(): pl.pallas_call(functools.partial(score_kernel, groups, tokens), out_shape...  16.3 us
    unnamed x1, local copies, waits for them, and re-layouts  0.6 us

profile of v3, /device:TPU:0, one launch (start us, length us, event | category | flops | bytes accessed | tf_op | source)
XLA Modules:
  0.0 16.9 jit_solution(1475725532749963918)
XLA Ops:
  0.0 16.3 %shard_map.46 = f32[8,128]{1,0:T(8,128)S(1)} custom-call(s32[8]{0:T(128)} %lens_hbm.1, bf16[256,128]{1,0:T(8,128)(2,1)} %bitcast.1, bf16[8,128,128]{2,1,0:T(8,128)(2,1)} %d_hbm.1, s32[8,128]{1,0:T(8,128)} %cand_hbm.1), custom_call_target="tpu_custom_call" | custom-call | tf_op jit(solution)/shard_map/pallas_call | solution.py:300
  16.3 0.6 %copy.6 = f32[8,128]{1,0:T(8,128)} copy(f32[8,128]{1,0:T(8,128)S(1)} %shard_map.46) | data formatting | bytes 8192

commit v4 on v3

--- a/solution.py
+++ b/solution.py
@@ -26,7 +26,7 @@
 
 
 def score_kernel(groups, tokens, lens_hbm, q_hbm, d_hbm, cand_hbm, out_ref,
-                 lens_ref, cand_ref, qbuf, dbuf, hbuf, best, rest_best, outgoing, pieces, extra,
+                 lens_ref, cand_ref, qbuf, dbuf, hbuf, best, rest_best, outgoing, whole, pieces, extra,
                  local_sem, here, q_send, q_recv, d_send, p_recv, y_recv, f_recv, o_send, o_recv, h_send, h_recv):
     part = lax.axis_index("parts")
     me = lax.axis_index("shard")
@@ -137,9 +137,9 @@
             sim = lax.dot_general(dbuf[which, j], block, (((1,), (1,)), ((), ())), preferred_element_type=jnp.float32)
             best[other[unit], which * docs + j:which * docs + j + 1, :] = jnp.max(sim, axis=0, keepdims=True)
 
-    def catch_up(have, ready, done):
+    def catch_up(have, units, done):
         for which in range(4):
-            for unit in ready:
+            for unit in units:
                 low = done.get((unit, which), 0)
                 if low < have[which]:
                     dot_max(unit, which, low, have[which])
@@ -163,7 +163,7 @@
     holder = jnp.where(source == g, k, 1 - k)
     near = lax.rem(device, 2) == holder
     local = jnp.where(same, jnp.where(near, 0, docs), jnp.where(near, 3 * docs, 2 * docs))
-    lane = lax.rem(cand, docs) + local
+    lane = lax.rem(g * per_unit, LANES) + lax.rem(cand, docs) + local
 
     q_of = lax.broadcasted_iota(jnp.int32, (count, q_rows), 1) // tokens
     pick = (q_of == lax.broadcasted_iota(jnp.int32, (count, q_rows), 0)).astype(jnp.float32)
@@ -181,7 +181,9 @@
     def widened(few):
         return jnp.concatenate([few, jnp.zeros((count, LANES - few.shape[1]), jnp.float32)], axis=1)
 
+    blocks = groups * per_unit // LANES
     results = {j: remote(outgoing.at[j], pieces.at[g], o_send, o_recv, level[j]) for j in order}
+    at_once = {j: remote(whole.at[other[j] * per_unit // LANES], pieces.at[g], o_send, o_recv, level[j]) for j in order}
 
     def run(plan):
         have, ready, done = [docs, 0, 0, 0], [0], {(0, 0): docs}
@@ -203,61 +205,71 @@
                 @pl.when(giver)
                 def _():
                     give.start()
-            else:
+            elif kind == "share":
+                @pl.when(home)
+                def _():
+                    give.wait_recv()
+                    share.start()
+            elif kind == "rest":
+                catch_up(have, ready, done)
+                total = means(best[...].reshape(groups * per_unit, q_rows))
+                for n in range(blocks):
+                    whole[n] = total[:, n * LANES:(n + 1) * LANES]
+                for j in order[::-1]:
+                    if j != which:
+                        at_once[j].start()
+                outgoing[0] = whole[g * per_unit // LANES]
+            elif kind in ("answer", "soon"):
                 def answer():
-                    outgoing[which] = widened(means(best[other[which]]))
+                    few = widened(means(best[other[which]]))
+                    if kind == "answer":
+                        few = pltpu.roll(few, lax.rem(other[which] * per_unit, LANES), 1)
+                    outgoing[which] = few
                     if which:
                         results[which].start()
 
-                if kind == "soon":
-                    pl.when(sooner)(answer)
-                elif short and which == 2 and now:
-                    pl.when(jnp.logical_not(sooner))(answer)
+                if now is True:
+                    answer()
                 else:
-                    answer()
+                    pl.when(now)(answer)
                 continue
             if now:
-                catch_up(have, ready, done)
-
+                catch_up(have, ready if now is True else now, done)
+
+    last = chunks - 1
     docs_first = [("p", 0, True)] + [("q", j, True) for j in order[:1]]
     for c in range(chunks):
         docs_first += [("y", c, True)] + [("r", c - 1, True)] * (c > 0)
-    docs_first.append(("r", chunks - 1, True))
-    docs_first += [("s", j, False) for j in order[:1]]
+    docs_first.append(("r", last, True))
+    docs_first += [("answer", j, True) for j in order[:1]]
     for j in order[1:]:
-        docs_first += [("q", j, True), ("s", j, False)]
-    docs_first.append(("s", 0, False))
-    docs_last = [("p", 0, True)]
-    for i in range(max(len(order), chunks)):
-        if i < chunks and i:
-            docs_last += [("r", i - 1, True)]
-            if short and i == chunks - 1:
-                docs_last += [("soon", 2, True)]
-            docs_last += [("y", i, i == 1)]
-        if i < len(order):
-            docs_last.append(("q", order[i], True))
-        if i < chunks and not i:
-            docs_last += [("y", i, True)] + [("give", 0, False)] * short
-    docs_last.append(("r", chunks - 1, True))
-    docs_last += [("s", j, True) for j in order[::-1] + [0]]
-    low = lax.rem(g, 4) < 2
-
-    @pl.when(low)
-    def _():
-        run(docs_first)
-
-    @pl.when(jnp.logical_not(low))
-    def _():
-        run(docs_last)
+        docs_first += [("q", j, True), ("answer", j, True)] + [("share", 0, False)] * (short and j == 2)
+    docs_first.append(("answer", 0, True))
+
+    def opening(hand):
+        return ([("p", 0, True)] + [("q", j, True) for j in order[:1]] + [("give", 0, False)] * hand
+                + [("y", 0, True)] + [step for c in range(1, last) for step in (("y", c, False), ("r", c - 1, True))]
+                + [("q", j, True) for j in order[1:2]] + [("y", last, False)])
+
+    far = [("q", j, True) for j in order[2:]]
+    if short:
+        third = opening(False) + far + [("r", last - 1, False), ("r", last, (3,)), ("soon", 3, True), ("rest", 3, False)]
+        fourth = opening(True) + [("r", last - 1, (2,)), ("soon", 2, sooner)] + far
+        fourth += [("r", last, (2,)), ("soon", 2, jnp.logical_not(sooner)), ("rest", 2, False)]
+        plans = [(lax.rem(g, 4) < 2, docs_first), (lax.rem(g, 4) == 2, third), (lax.rem(g, 4) == 3, fourth)]
+    else:
+        plans = [(True, docs_first)]
+    for when, plan in plans:
+        if when is True:
+            run(plan)
+        else:
+            pl.when(when)(functools.partial(run, plan))
 
     if short:
         @pl.when(home)
         def _():
-            give.wait_recv()
-            share.start()
+            share.wait_recv()
             for n in range(2):
-                if n:
-                    share.wait_recv()
                 for j in range(tail):
                     sim = lax.dot_general(hbuf[n, j], qbuf[g], (((1,), (1,)), ((), ())), preferred_element_type=jnp.float32)
                     rest_best[n * tail + j:n * tail + j + 1, :] = jnp.max(sim, axis=0, keepdims=True)
@@ -284,8 +296,8 @@
         back.wait_send()
     if short:
         row = lax.rem(cand, docs) - late
-        whole = (source == top) & jnp.logical_not(same) & (row >= 0) & home
-        out = jnp.where(whole, picked(extra[...], jnp.where(whole, row + jnp.where(near, 0, tail), 0)), out)
+        mine_whole = (source == top) & jnp.logical_not(same) & (row >= 0) & home
+        out = jnp.where(mine_whole, picked(extra[...], jnp.where(mine_whole, row + jnp.where(near, 0, tail), 0)), out)
     out_ref[...] = out
 
 
@@ -296,6 +308,7 @@
     chunks = len(cut_points(docs)) - 1
     tail = docs - cut_points(docs)[-2]
     q_rows = count * tokens
+    blocks = groups * 4 * docs // LANES
     dma = pltpu.SemaphoreType.DMA
     return pl.pallas_call(
         functools.partial(score_kernel, groups, tokens),
@@ -311,6 +324,7 @@
             pltpu.VMEM((groups, 4 * docs, q_rows), jnp.float32),
             pltpu.VMEM((2 * tail, q_rows), jnp.float32),
             pltpu.VMEM((groups, count, LANES), jnp.float32),
+            pltpu.VMEM((blocks, count, LANES), jnp.float32),
             pltpu.VMEM((groups, count, LANES), jnp.float32),
             pltpu.VMEM((count, LANES), jnp.float32),
             dma((4,)),

time: 17.1 us -> 16.8 us (0.982)
  Pallas kernels: 16.3 us -> 16 us
    pallas_call x1, Pallas kernels: 16.3 us -> 16 us  [body(): pl.pallas_call(functools.partial(score_kernel, groups, tokens), out_shape...]
where the time goes in v4:
time: 16.8 us; the launch traced here: 16.6 us
  Pallas kernels  16 us (95%)
  local copies, waits for them, and re-layouts  0.6 us (4%)
    pallas_call x1, Pallas kernels, body(): pl.pallas_call(functools.partial(score_kernel, groups, tokens), out_shape...  16 us
    unnamed x1, local copies, waits for them, and re-layouts  0.6 us

profile of v4, /device:TPU:0, one launch (start us, length us, event | category | flops | bytes accessed | tf_op | source)
XLA Modules:
  0.0 16.6 jit_solution(2676271886699062247)
XLA Ops:
  0.0 16.0 %shard_map.46 = f32[8,128]{1,0:T(8,128)S(1)} custom-call(s32[8]{0:T(128)} %lens_hbm.1, bf16[256,128]{1,0:T(8,128)(2,1)} %bitcast.1, bf16[8,128,128]{2,1,0:T(8,128)(2,1)} %d_hbm.1, s32[8,128]{1,0:T(8,128)} %cand_hbm.1), custom_call_target="tpu_custom_call" | custom-call | tf_op jit(solution)/shard_map/pallas_call | solution.py:313
  16.0 0.6 %copy.6 = f32[8,128]{1,0:T(8,128)} copy(f32[8,128]{1,0:T(8,128)S(1)} %shard_map.46) | data formatting | bytes 8192

commit v5 on v4

--- a/solution.py
+++ b/solution.py
@@ -22,7 +22,7 @@
 
 
 def cut_points(docs):
-    return [0, docs // 2, docs - docs // 4, docs]
+    return [0, 3, 5, 8]
 
 
 def score_kernel(groups, tokens, lens_hbm, q_hbm, d_hbm, cand_hbm, out_ref,
@@ -149,9 +149,18 @@
         meet(2)
         q_out[order[0]].start()
     dot_max(0, 0, 0, docs)
-    for i, j in enumerate(order[1:]):
-        meet(3 + i)
-        q_out[j].start()
+    swapped = lax.rem(g, 4) == 2
+    for j in order[1:]:
+        out_mask, out_level = mask[j], other[j]
+        if short and j % 4 > 1:
+            out_mask = jnp.where(swapped, mask[j ^ 1], out_mask)
+            out_level = jnp.where(swapped, other[j ^ 1], out_level)
+
+        @pl.when(g < out_level)
+        def _():
+            pl.semaphore_wait(here.at[1 + out_mask], 1)
+
+        remote(mine, mine, q_send, q_recv.at[out_mask - 1], at(out_level, b, 1 - k)).start()
 
     give = remote(dbuf.at[0, pl.ds(late, tail)], hbuf.at[0], h_send, h_recv.at[0], at(top, 0, 1 - k))
     share = remote(hbuf.at[0], hbuf.at[1], h_send, h_recv.at[1], partner)
@@ -242,9 +251,9 @@
         docs_first += [("y", c, True)] + [("r", c - 1, True)] * (c > 0)
     docs_first.append(("r", last, True))
     docs_first += [("answer", j, True) for j in order[:1]]
-    for j in order[1:]:
-        docs_first += [("q", j, True), ("answer", j, True)] + [("share", 0, False)] * (short and j == 2)
-    docs_first.append(("answer", 0, True))
+    for j in order[2:] + order[1:2]:
+        docs_first += [("q", j, True), ("answer", j, True)]
+    docs_first += [("share", 0, False)] * short + [("answer", 0, True)]
 
     def opening(hand):
         return ([("p", 0, True)] + [("q", j, True) for j in order[:1]] + [("give", 0, False)] * hand

time: 16.8 us -> 16.5 us (0.982)
  Pallas kernels: 16 us -> 15.7 us
    pallas_call x1, Pallas kernels: 16 us -> 15.7 us  [body(): pl.pallas_call(functools.partial(score_kernel, groups, tokens), out_shape...]
where the time goes in v5:
time: 16.5 us; the launch traced here: 16.3 us
  Pallas kernels  15.7 us (95%)
  local copies, waits for them, and re-layouts  0.6 us (4%)
    pallas_call x1, Pallas kernels, body(): pl.pallas_call(functools.partial(score_kernel, groups, tokens), out_shape...  15.7 us
    unnamed x1, local copies, waits for them, and re-layouts  0.6 us

profile of v5, /device:TPU:0, one launch (start us, length us, event | category | flops | bytes accessed | tf_op | source)
XLA Modules:
  0.0 16.3 jit_solution(6200901302389274253)
XLA Ops:
  0.0 15.7 %shard_map.46 = f32[8,128]{1,0:T(8,128)S(1)} custom-call(s32[8]{0:T(128)} %lens_hbm.1, bf16[256,128]{1,0:T(8,128)(2,1)} %bitcast.1, bf16[8,128,128]{2,1,0:T(8,128)(2,1)} %d_hbm.1, s32[8,128]{1,0:T(8,128)} %cand_hbm.1), custom_call_target="tpu_custom_call" | custom-call | tf_op jit(solution)/shard_map/pallas_call | solution.py:322
  15.7 0.6 %copy.6 = f32[8,128]{1,0:T(8,128)} copy(f32[8,128]{1,0:T(8,128)S(1)} %shard_map.46) | data formatting | bytes 8192

commit v6 on v5

--- a/solution.py
+++ b/solution.py
@@ -255,14 +255,14 @@
         docs_first += [("q", j, True), ("answer", j, True)]
     docs_first += [("share", 0, False)] * short + [("answer", 0, True)]
 
-    def opening(hand):
-        return ([("p", 0, True)] + [("q", j, True) for j in order[:1]] + [("give", 0, False)] * hand
+    def opening(hand, early=False):
+        return ([("p", 0, True)] + [("give", 0, False)] * hand + [("q", j, True) for j in order[:1]]
                 + [("y", 0, True)] + [step for c in range(1, last) for step in (("y", c, False), ("r", c - 1, True))]
-                + [("q", j, True) for j in order[1:2]] + [("y", last, False)])
+                + [("y", last, False)] * early + [("q", j, True) for j in order[1:2]] + [("y", last, False)] * (not early))
 
     far = [("q", j, True) for j in order[2:]]
     if short:
-        third = opening(False) + far + [("r", last - 1, False), ("r", last, (3,)), ("soon", 3, True), ("rest", 3, False)]
+        third = opening(False, True)[:-1] + [("q", 2, False)] + [("q", 3, (3,))] + [("r", last - 1, False), ("r", last, (3,)), ("soon", 3, True), ("rest", 3, False)]
         fourth = opening(True) + [("r", last - 1, (2,)), ("soon", 2, sooner)] + far
         fourth += [("r", last, (2,)), ("soon", 2, jnp.logical_not(sooner)), ("rest", 2, False)]
         plans = [(lax.rem(g, 4) < 2, docs_first), (lax.rem(g, 4) == 2, third), (lax.rem(g, 4) == 3, fourth)]

time: 16.5 us -> 16.3 us (0.988)
  no operation moved by 1% of the time
where the time goes in v6:
time: 16.3 us; the launch traced here: 16.2 us
  Pallas kernels  15.6 us (96%)
  local copies, waits for them, and re-layouts  0.6 us (4%)
    pallas_call x1, Pallas kernels, body(): pl.pallas_call(functools.partial(score_kernel, groups, tokens), out_shape...  15.6 us
    unnamed x1, local copies, waits for them, and re-layouts  0.6 us

profile of v6, /device:TPU:0, one launch (start us, length us, event | category | flops | bytes accessed | tf_op | source)
XLA Modules:
  0.0 16.2 jit_solution(10948760018998948949)
XLA Ops:
  0.0 15.6 %shard_map.46 = f32[8,128]{1,0:T(8,128)S(1)} custom-call(s32[8]{0:T(128)} %lens_hbm.1, bf16[256,128]{1,0:T(8,128)(2,1)} %bitcast.1, bf16[8,128,128]{2,1,0:T(8,128)(2,1)} %d_hbm.1, s32[8,128]{1,0:T(8,128)} %cand_hbm.1), custom_call_target="tpu_custom_call" | custom-call | tf_op jit(solution)/shard_map/pallas_call | solution.py:322
  15.6 0.6 %copy.6 = f32[8,128]{1,0:T(8,128)} copy(f32[8,128]{1,0:T(8,128)S(1)} %shard_map.46) | data formatting | bytes 8192

commit v7 on v6

--- a/solution.py
+++ b/solution.py
@@ -150,7 +150,14 @@
         q_out[order[0]].start()
     dot_max(0, 0, 0, docs)
     swapped = lax.rem(g, 4) == 2
+    give = remote(dbuf.at[0, pl.ds(late, tail)], hbuf.at[0], h_send, h_recv.at[0], at(top, 0, 1 - k))
+    share = remote(hbuf.at[0], hbuf.at[1], h_send, h_recv.at[1], partner)
     for j in order[1:]:
+        if short and j == 3:
+            @pl.when(jnp.logical_and(giver, k == 0))
+            def _():
+                give.start()
+
         out_mask, out_level = mask[j], other[j]
         if short and j % 4 > 1:
             out_mask = jnp.where(swapped, mask[j ^ 1], out_mask)
@@ -162,8 +169,6 @@
 
         remote(mine, mine, q_send, q_recv.at[out_mask - 1], at(out_level, b, 1 - k)).start()
 
-    give = remote(dbuf.at[0, pl.ds(late, tail)], hbuf.at[0], h_send, h_recv.at[0], at(top, 0, 1 - k))
-    share = remote(hbuf.at[0], hbuf.at[1], h_send, h_recv.at[1], partner)
     cand_in.wait()
     cand = cand_ref[...]
     device = cand // docs
@@ -211,7 +216,7 @@
                 relays[which].wait_recv()
                 have[3] = edges[which + 1]
             elif kind == "give":
-                @pl.when(giver)
+                @pl.when(jnp.logical_and(giver, k == 1))
                 def _():
                     give.start()
             elif kind == "share":
@@ -263,9 +268,11 @@
     far = [("q", j, True) for j in order[2:]]
     if short:
         third = opening(False, True)[:-1] + [("q", 2, False)] + [("q", 3, (3,))] + [("r", last - 1, False), ("r", last, (3,)), ("soon", 3, True), ("rest", 3, False)]
-        fourth = opening(True) + [("r", last - 1, (2,)), ("soon", 2, sooner)] + far
-        fourth += [("r", last, (2,)), ("soon", 2, jnp.logical_not(sooner)), ("rest", 2, False)]
-        plans = [(lax.rem(g, 4) < 2, docs_first), (lax.rem(g, 4) == 2, third), (lax.rem(g, 4) == 3, fourth)]
+        fourth = opening(True) + [("r", last - 1, False)] + far
+        fourth += [("r", last, (2,)), ("soon", 2, True), ("rest", 2, False)]
+        soonest = opening(False)[:-2] + [("q", 2, (2,)), ("r", last - 1, (2,)), ("soon", 2, True), ("y", last, False)] + far
+        soonest += [("r", last, False), ("rest", 2, False)]
+        plans = [(lax.rem(g, 4) < 2, docs_first), (lax.rem(g, 4) == 2, third), (giver, fourth), (sooner, soonest)]
     else:
         plans = [(True, docs_first)]
     for when, plan in plans:
@@ -277,8 +284,9 @@
     if short:
         @pl.when(home)
         def _():
-            share.wait_recv()
             for n in range(2):
+                if n:
+                    share.wait_recv()
                 for j in range(tail):
                     sim = lax.dot_general(hbuf[n, j], qbuf[g], (((1,), (1,)), ((), ())), preferred_element_type=jnp.float32)
                     rest_best[n * tail + j:n * tail + j + 1, :] = jnp.max(sim, axis=0, keepdims=True)
@@ -297,6 +305,10 @@
     out = picked(outgoing[0], lane)
     for copy in sent:
         copy.wait_send()
+    if short:
+        row = lax.rem(cand, docs) - late
+        mine_whole = (source == top) & jnp.logical_not(same) & (row >= 0) & home
+        given = picked(extra[...], jnp.where(mine_whole, row + jnp.where(near, 0, tail), 0))
     if order:
         back = remote(pieces.at[pl.ds(0, groups - 1)], pieces.at[pl.ds(0, groups - 1)], o_send, o_recv, partner)
         back.wait_recv()
@@ -304,9 +316,7 @@
             out = jnp.where(source == other[j], picked(pieces[other[j]], lane), out)
         back.wait_send()
     if short:
-        row = lax.rem(cand, docs) - late
-        mine_whole = (source == top) & jnp.logical_not(same) & (row >= 0) & home
-        out = jnp.where(mine_whole, picked(extra[...], jnp.where(mine_whole, row + jnp.where(near, 0, tail), 0)), out)
+        out = jnp.where(mine_whole, given, out)
     out_ref[...] = out
 
 

time: 16.3 us -> 16 us (0.982)
  Pallas kernels: 15.6 us -> 15.2 us
    pallas_call x1, Pallas kernels: 15.6 us -> 15.2 us  [body(): pl.pallas_call(functools.partial(score_kernel, groups, tokens), out_shape...]
where the time goes in v7:
time: 16 us; the launch traced here: 15.8 us
  Pallas kernels  15.2 us (95%)
  local copies, waits for them, and re-layouts  0.6 us (4%)
    pallas_call x1, Pallas kernels, body(): pl.pallas_call(functools.partial(score_kernel, groups, tokens), out_shape...  15.2 us
    unnamed x1, local copies, waits for them, and re-layouts  0.6 us

profile of v7, /device:TPU:0, one launch (start us, length us, event | category | flops | bytes accessed | tf_op | source)
XLA Modules:
  0.0 15.8 jit_solution(12355363831827447903)
XLA Ops:
  0.0 15.2 %shard_map.46 = f32[8,128]{1,0:T(8,128)S(1)} custom-call(s32[8]{0:T(128)} %lens_hbm.1, bf16[256,128]{1,0:T(8,128)(2,1)} %bitcast.1, bf16[8,128,128]{2,1,0:T(8,128)(2,1)} %d_hbm.1, s32[8,128]{1,0:T(8,128)} %cand_hbm.1), custom_call_target="tpu_custom_call" | custom-call | tf_op jit(solution)/shard_map/pallas_call | solution.py:332
  15.2 0.6 %copy.6 = f32[8,128]{1,0:T(8,128)} copy(f32[8,128]{1,0:T(8,128)S(1)} %shard_map.46) | data formatting | bytes 8192

commit v8 on v7

--- a/solution.py
+++ b/solution.py
@@ -22,7 +22,7 @@
 
 
 def cut_points(docs):
-    return [0, 3, 5, 8]
+    return [0, docs * 3 // 8, docs * 5 // 8, docs]
 
 
 def score_kernel(groups, tokens, lens_hbm, q_hbm, d_hbm, cand_hbm, out_ref,
@@ -267,7 +267,8 @@
 
     far = [("q", j, True) for j in order[2:]]
     if short:
-        third = opening(False, True)[:-1] + [("q", 2, False)] + [("q", 3, (3,))] + [("r", last - 1, False), ("r", last, (3,)), ("soon", 3, True), ("rest", 3, False)]
+        third = opening(False, True)[:-1] + [("q", 2, False)] + [("q", 3, (3,))] + [("r", last - 1, False), ("r", last, (3,)), ("soon", 3, True)]
+        third += [("q", j, False) for j in order[3:]] + [("rest", 3, False)]
         fourth = opening(True) + [("r", last - 1, False)] + far
         fourth += [("r", last, (2,)), ("soon", 2, True), ("rest", 2, False)]
         soonest = opening(False)[:-2] + [("q", 2, (2,)), ("r", last - 1, (2,)), ("soon", 2, True), ("y", last, False)] + far

time: 16 us -> 16 us (level)
  no operation moved by 1% of the time
where the time goes in v8:
time: 16 us; the launch traced here: 15.8 us
  Pallas kernels  15.2 us (95%)
  local copies, waits for them, and re-layouts  0.6 us (4%)
    pallas_call x1, Pallas kernels, body(): pl.pallas_call(functools.partial(score_kernel, groups, tokens), out_shape...  15.2 us
    unnamed x1, local copies, waits for them, and re-layouts  0.6 us

profile of v8, /device:TPU:0, one launch (start us, length us, event | category | flops | bytes accessed | tf_op | source)
XLA Modules:
  0.0 15.8 jit_solution(12355363831827447903)
XLA Ops:
  0.0 15.2 %shard_map.46 = f32[8,128]{1,0:T(8,128)S(1)} custom-call(s32[8]{0:T(128)} %lens_hbm.1, bf16[256,128]{1,0:T(8,128)(2,1)} %bitcast.1, bf16[8,128,128]{2,1,0:T(8,128)(2,1)} %d_hbm.1, s32[8,128]{1,0:T(8,128)} %cand_hbm.1), custom_call_target="tpu_custom_call" | custom-call | tf_op jit(solution)/shard_map/pallas_call | solution.py:333
  15.2 0.6 %copy.6 = f32[8,128]{1,0:T(8,128)} copy(f32[8,128]{1,0:T(8,128)S(1)} %shard_map.46) | data formatting | bytes 8192
